TPU v7x, 16 devices: a whole 2x2x2 slice. The times are simulated.
16 devices in a mesh: dp: 2 (over z), tp: 8 (over y, x, core).
Axes of the slice: x: 2, y: 2, z: 2, core: 2. Of those that a mesh axis runs over, the one named last changes fastest.
Arguments:
- x_in: bfloat16 [2048, 4096], P('dp'), parts along dimension 0
- h_mid: bfloat16 [2048, 4096], P('dp'), parts along dimension 0
- mean_x: float32 [2048], P('dp'), parts along dimension 0
- rstd_x: float32 [2048], P('dp'), parts along dimension 0
- mean_h: float32 [2048], P('dp'), parts along dimension 0
- rstd_h: float32 [2048], P('dp'), parts along dimension 0
- gain_x: bfloat16 [4096], replicated
- gain_h: bfloat16 [4096], replicated
- w_qkv: bfloat16 [4096, 6144], P(None, 'tp')
- w_out: bfloat16 [32, 128, 4096], P('tp')
- w_gate: bfloat16 [4096, 14336], P(None, 'tp')
- w_up: bfloat16 [4096, 14336], P(None, 'tp')
- w_down: bfloat16 [14336, 4096], P('tp')
- d_out: bfloat16 [2048, 4096], P('dp'), parts along dimension 0
Outputs:
- output 1: bfloat16 [2048, 4096], P('dp'), parts along dimension 0
- output 2: bfloat16 [8192, 6144], P('dp', 'tp'), parts along dimension 0
- output 3: bfloat16 [64, 128, 4096], P(('dp', 'tp')), parts along dimension 0
- output 4: bfloat16 [8192, 14336], P('dp', 'tp'), parts along dimension 0
- output 5: bfloat16 [8192, 14336], P('dp', 'tp'), parts along dimension 0
- output 6: bfloat16 [28672, 4096], P(('dp', 'tp')), parts along dimension 0
There are 2 independent parts. A program takes and returns all parts, laid end to end along the dimension named above; an argument that names none is the same for every part.
All inputs are finite; a program needn't handle non-finite values.
Results may differ from a plain program's by a relative error of at most 0.0159252.
Values are sent between devices in bfloat16 or wider.
A program may use at most 1 GiB of HBM per device.

v0:
```python
import jax
import jax.numpy as jnp
from jax import lax
from jax.sharding import PartitionSpec as P


def layer_norm(src_rows, row_mean, row_rstd, gain_vec):
    centred = (src_rows.astype(jnp.float32) - row_mean[..., None]) * row_rstd[..., None]
    return (centred * gain_vec.astype(jnp.float32)).astype(jnp.bfloat16)


def norm_backward(grad_n, src_rows, row_mean, row_rstd, gain_vec):
    centred = (src_rows.astype(jnp.float32) - row_mean[..., None]) * row_rstd[..., None]
    scaled = grad_n * gain_vec.astype(jnp.float32)
    mean_grad = jnp.mean(scaled, axis=-1, keepdims=True)
    mean_proj = jnp.mean(scaled * centred, axis=-1, keepdims=True)
    return row_rstd[..., None] * (scaled - mean_grad - centred * mean_proj)


def local_attention(qkv_rows, d_heads):
    group_size = qkv_rows.shape[2] - 2
    queries = qkv_rows[:, :, :group_size]
    key_rows = qkv_rows[:, :, group_size]
    value_rows = qkv_rows[:, :, group_size + 1]
    score_scale = qkv_rows.shape[3] ** -0.5
    positions = jnp.arange(qkv_rows.shape[0])
    causal = positions[:, None] >= positions[None, :]
    scores = jnp.einsum('tkgd,skd->kgts', queries, key_rows, preferred_element_type=jnp.float32) * score_scale
    attn_probs = jax.nn.softmax(jnp.where(causal, scores, -1e30), axis=-1)
    probs_low = attn_probs.astype(jnp.bfloat16)
    outputs = jnp.einsum('kgts,skd->tkgd', probs_low, value_rows, preferred_element_type=jnp.float32).astype(jnp.bfloat16)
    d_probs = jnp.einsum('tkgd,skd->kgts', d_heads, value_rows, preferred_element_type=jnp.float32)
    row_dot = jnp.sum(attn_probs * d_probs, axis=-1, keepdims=True)
    d_scores = (attn_probs * (d_probs - row_dot) * score_scale).astype(jnp.bfloat16)
    grad_q = jnp.einsum('kgts,skd->tkgd', d_scores, key_rows, preferred_element_type=jnp.float32)
    grad_k = jnp.einsum('kgts,tkgd->skd', d_scores, queries, preferred_element_type=jnp.float32)
    grad_v = jnp.einsum('kgts,tkgd->skd', probs_low, d_heads, preferred_element_type=jnp.float32)
    d_qkv = jnp.concatenate([grad_q, grad_k[:, :, None], grad_v[:, :, None]], axis=2)
    return outputs, d_qkv.astype(jnp.bfloat16)


def solution(mesh):
    def device_step(x_in, h_mid, mean_x, rstd_x, mean_h, rstd_h, gain_x, gain_h, w_qkv, w_out, w_gate, w_up, w_down, d_out):
        heads_local, head_dim = w_out.shape[0], w_out.shape[1]
        kv_local = (w_qkv.shape[1] // head_dim - heads_local) // 2
        group_size = heads_local // kv_local
        tokens = x_in.shape[0]
        norm_h = layer_norm(h_mid, mean_h, rstd_h, gain_h)
        gate_f = jnp.dot(norm_h, w_gate, preferred_element_type=jnp.float32).astype(jnp.bfloat16).astype(jnp.float32)
        up_f = jnp.dot(norm_h, w_up, preferred_element_type=jnp.float32).astype(jnp.bfloat16).astype(jnp.float32)
        sig_gate = jax.nn.sigmoid(gate_f)
        gate_act = gate_f * sig_gate
        hidden = (gate_act * up_f).astype(jnp.bfloat16)
        d_w_down = jnp.einsum('tf,te->fe', hidden, d_out, preferred_element_type=jnp.float32).astype(jnp.bfloat16)
        d_hidden = jnp.einsum('te,fe->tf', d_out, w_down, preferred_element_type=jnp.float32).astype(jnp.bfloat16).astype(jnp.float32)
        d_gate = (d_hidden * up_f * sig_gate * (1.0 + gate_f * (1.0 - sig_gate))).astype(jnp.bfloat16)
        d_up = (d_hidden * gate_act).astype(jnp.bfloat16)
        d_w_gate = jnp.einsum('td,tf->df', norm_h, d_gate, preferred_element_type=jnp.float32).astype(jnp.bfloat16)
        d_w_up = jnp.einsum('td,tf->df', norm_h, d_up, preferred_element_type=jnp.float32).astype(jnp.bfloat16)
        part_h = jnp.einsum('tf,df->td', d_gate, w_gate, preferred_element_type=jnp.float32) + jnp.einsum('tf,df->td', d_up, w_up, preferred_element_type=jnp.float32)
        d_norm_h = lax.psum(part_h.astype(jnp.bfloat16), 'tp').astype(jnp.float32)
        d_mid = d_out.astype(jnp.float32) + norm_backward(d_norm_h, h_mid, mean_h, rstd_h, gain_h)
        d_mid_b = d_mid.astype(jnp.bfloat16)
        norm_x = layer_norm(x_in, mean_x, rstd_x, gain_x)
        qkv_rows = jnp.dot(norm_x, w_qkv, preferred_element_type=jnp.float32).astype(jnp.bfloat16)
        qkv_rows = qkv_rows.reshape(tokens, kv_local, group_size + 2, head_dim)
        d_heads = jnp.einsum('te,hze->thz', d_mid_b, w_out, preferred_element_type=jnp.float32).astype(jnp.bfloat16)
        outputs, d_qkv = local_attention(qkv_rows, d_heads.reshape(tokens, kv_local, group_size, head_dim))
        d_w_out = jnp.einsum('thz,te->hze', outputs.reshape(tokens, heads_local, head_dim), d_mid_b, preferred_element_type=jnp.float32).astype(jnp.bfloat16)
        d_qkv = d_qkv.reshape(tokens, w_qkv.shape[1])
        d_w_qkv = jnp.einsum('td,tc->dc', norm_x, d_qkv, preferred_element_type=jnp.float32).astype(jnp.bfloat16)
        part_x = jnp.einsum('tc,dc->td', d_qkv, w_qkv, preferred_element_type=jnp.float32)
        d_norm_x = lax.psum(part_x.astype(jnp.bfloat16), 'tp').astype(jnp.float32)
        d_x = (d_mid + norm_backward(d_norm_x, x_in, mean_x, rstd_x, gain_x)).astype(jnp.bfloat16)
        return d_x, d_w_qkv, d_w_out, d_w_gate, d_w_up, d_w_down

    row_spec = P('dp', None)
    stat_spec = P('dp')
    col_spec = P(None, 'tp')
    in_specs = (row_spec, row_spec, stat_spec, stat_spec, stat_spec, stat_spec, P(None), P(None), col_spec, P('tp', None, None), col_spec, col_spec, P('tp', None), row_spec)
    out_specs = (row_spec, P('dp', 'tp'), P(('dp', 'tp'), None, None), P('dp', 'tp'), P('dp', 'tp'), P(('dp', 'tp'), None))
    return jax.shard_map(device_step, mesh=mesh, in_specs=in_specs, out_specs=out_specs, check_vma=False)
```

profile of v0, /device:TPU:0, one launch (start us, length us, event | category | flops | bytes accessed | tf_op | source)
XLA Modules:
  0.0 474.9 jit_solution(4734643361588904501)
XLA Ops:
  7.9 23.4 %convolution_convert_fusion.6 = bf16[1024,1792]{1,0:T(8,128)(2,1)} fusion(bf16[4096,1792]{1,0:T(8,128)(2,1)} %param.25, bf16[1024,4096]{1,0:T(8,128)(2,1)} %param.15, f32[4096]{0:T(1024)S(1)} %convert_element_type.117, f32[1024]{0:T(1024)} %param.18, f32[1024]{0:T(1024)} %param.19), kind=kOutput, calls=%fused_computation.59 | convolution fusion | flops 15055192064 | bytes 26763264 | tf_op jit(solution)/shard_map/dot_general | solution.py:50
  31.3 17.2 %convolution_convert_fusion.5 = bf16[1024,1792]{1,0:T(8,128)(2,1)} fusion(bf16[4096,1792]{1,0:T(8,128)(2,1)S(1)} %copy-done.21, bf16[1024,4096]{1,0:T(8,128)(2,1)S(1)} %copy-done.1, f32[4096]{0:T(1024)S(1)} %convert_element_type.117, f32[1024]{0:T(1024)S(1)} %copy-done.14, f32[1024]{0:T(1024)S(1)} %copy-done.15), kind=kOutput, calls=%fused_computation.58 | convolution fusion | flops 15055192064 | bytes 26763264 | tf_op jit(solution)/shard_map/dot_general | solution.py:49
  48.6 22.9 %convolution_convert_fusion.7 = bf16[1024,1792]{1,0:T(8,128)(2,1)} fusion(bf16[1024,4096]{1,0:T(8,128)(2,1)} %param.27, bf16[1792,4096]{1,0:T(8,128)(2,1)} %param.26), kind=kOutput, calls=%fused_computation.60 | convolution fusion | flops 15034220544 | bytes 26738688 | tf_op jit(solution)/shard_map/te,fe->tf/dot_general | solution.py:55
  71.5 29.4 %fusion.66 = f32[1024,4096]{1,0:T(8,128)} fusion(bf16[4096,1792]{1,0:T(8,128)(2,1)} %param.24, bf16[1024,1792]{1,0:T(8,128)(2,1)} %convolution_convert_fusion.6, bf16[1024,1792]{1,0:T(8,128)(2,1)} %convolution_convert_fusion.7, bf16[1024,1792]{1,0:T(8,128)(2,1)} %convolution_convert_fusion.5), kind=kOutput, calls=%fused_computation.84 | convolution fusion | flops 15056240640 | bytes 42467328 | tf_op jit(solution)/shard_map/tf,df->td/dot_general | solution.py:60
  100.9 27.1 %add_convert_fusion.1 = bf16[1024,4096]{1,0:T(8,128)(2,1)} fusion(f32[1024,4096]{1,0:T(8,128)} %fusion.66, bf16[4096,1792]{1,0:T(8,128)(2,1)} %param.25, bf16[1024,1792]{1,0:T(8,128)(2,1)} %convolution_convert_fusion.7, bf16[1024,1792]{1,0:T(8,128)(2,1)} %convolution_convert_fusion.5), kind=kOutput, calls=%fused_computation.18 | convolution fusion | flops 15055454208 | bytes 47185920 | tf_op jit(solution)/shard_map/tf,df->td/dot_general | solution.py:60
  128.4 27.3 %convolution_convert_fusion.2 = bf16[4096,1792]{1,0:T(8,128)(2,1)} fusion(bf16[1024,1792]{1,0:T(8,128)(2,1)} %convolution_convert_fusion.6, bf16[1024,1792]{1,0:T(8,128)(2,1)} %convolution_convert_fusion.7, bf16[1024,1792]{1,0:T(8,128)(2,1)} %convolution_convert_fusion.5, bf16[1024,4096]{1,0:T(8,128)(2,1)} %param.15, f32[4096]{0:T(1024)S(1)} %convert_element_type.117, ...), kind=kOutput, calls=%fused_computation.23 | convolution fusion | flops 15084552192 | bytes 34103296 | tf_op jit(solution)/shard_map/td,tf->df/dot_general | solution.py:58
  155.7 24.0 %convolution_convert_fusion = bf16[1792,4096]{1,0:T(8,128)(2,1)} fusion(bf16[1024,4096]{1,0:T(8,128)(2,1)} %param.27, bf16[1024,1792]{1,0:T(8,128)(2,1)} %convolution_convert_fusion.6, bf16[1024,1792]{1,0:T(8,128)(2,1)} %convolution_convert_fusion.5), kind=kOutput, calls=%fused_computation.21 | convolution fusion | flops 15054405632 | bytes 30408704 | tf_op jit(solution)/shard_map/tf,te->fe/dot_general | solution.py:54
  179.7 11.9 %convolution_convert_fusion.8 = bf16[1024,768]{0,1:T(8,128)(2,1)S(1)} fusion(bf16[4096,768]{1,0:T(8,128)(2,1)} %param.22, bf16[1024,4096]{1,0:T(8,128)(2,1)} %param.14, f32[4096]{0:T(1024)S(1)} %convert_element_type.128, f32[1024]{0:T(1024)S(1)} %copy-done.16, f32[1024]{0:T(1024)S(1)} %copy-done.18), kind=kOutput, calls=%fused_computation.61 | convolution fusion | flops 6464208896 | bytes 16277504 | tf_op jit(solution)/shard_map/dot_general | solution.py:65
  195.1 5.7 %copy-done = f32[1024,1024,4]{1,0,2:T(8,128)} copy-done((f32[1024,1024,4]{1,0,2:T(8,128)}, f32[1024,1024,4]{1,0,2:T(8,128)S(1)}, u32[]{:S(2)}) %copy-start) | copy-done | bytes 16777240
  200.8 4.3 fusion.7
  205.1 24.9 %convolution_convert_fusion.1 = bf16[4096,1792]{1,0:T(8,128)(2,1)} fusion(bf16[1024,1792]{1,0:T(8,128)(2,1)} %convolution_convert_fusion.7, bf16[1024,1792]{1,0:T(8,128)(2,1)} %convolution_convert_fusion.5, bf16[1024,4096]{1,0:T(8,128)(2,1)} %param.15, f32[4096]{0:T(1024)S(1)} %convert_element_type.117, f32[1024]{0:T(1024)S(1)} %copy-done.14, ...), kind=kOutput, calls=%fused_computation.22 | convolution fusion | flops 15075377152 | bytes 30433280 | tf_op jit(solution)/shard_map/td,tf->df/dot_general | solution.py:59
  230.0 19.2 %all-reduce.3.cloned.1.call-done = bf16[1024,4096]{1,0:T(8,128)(2,1)} async-done(((bf16[1024,4096]{1,0:T(8,128)(2,1)}), bf16[1024,4096]{1,0:T(8,128)(2,1)}) %all-reduce.3.cloned.1.call-update) | async-done | bytes 8388624 | tf_op jit(solution)/shard_map/psum | solution.py:61
  249.3 8.9 %fusion.5 = (f32[1024]{0:T(1024)S(1)}, f32[1024]{0:T(1024)S(1)}) fusion(bf16[1024,4096]{1,0:T(8,128)(2,1)} %all-reduce.3.cloned.1.call-done, f32[4096]{0:T(1024)S(1)} %convert_element_type.117, f32[1024]{0:T(1024)S(1)} %copy-done.15, f32[1024]{0:T(1024)S(1)} %copy-done.14, bf16[1024,4096]{1,0:T(8,128)(2,1)} %param.15), kind=kLoop, calls=%fused_computation.17 | loop fusion | flops 33552384 | bytes 16809984 | tf_op jit(solution)/shard_map/reduce_sum | solution.py:15
  258.2 16.4 %multiply_add_fusion = f32[1024,4096]{1,0:T(8,128)} fusion(bf16[1024,4096]{1,0:T(8,128)(2,1)S(1)} %copy-done.2, bf16[1024,4096]{1,0:T(8,128)(2,1)} %param.15, bf16[1024,4096]{1,0:T(8,128)(2,1)} %param.27, f32[1024]{0:T(1024)S(1)} %get-tuple-element.14, f32[1024]{0:T(1024)S(1)} %get-tuple-element.15, f32[4096]{0:T(1024)S(1)} %convert_element_type.117, ...), kind=kLoop, calls=%fused_computation.14 | loop fusion | flops 46137344 | bytes 41975808 | tf_op jit(solution)/shard_map/add | solution.py:62
  274.6 9.5 %fusion.34 = bf16[1024,4,128]{2,0,1:T(8,128)(2,1)S(1)} fusion(bf16[4,128,4096]{2,1,0:T(8,128)(2,1)} %param.23, f32[1024,4096]{1,0:T(8,128)} %multiply_add_fusion), kind=kOutput, calls=%fused_computation.63 | convolution fusion | flops 4299685888 | bytes 22020096 | tf_op jit(solution)/shard_map/te,hze->thz/dot_general | solution.py:67
  285.1 6.3 %fusion.51 = bf16[1024,1,1,128]{0,3,2,1:T(8,128)(2,1)} fusion(bf16[1024,4,128]{2,0,1:T(8,128)(2,1)S(1)} %fusion.34, f32[4,1024]{1,0:T(4,128)S(1)} %copy-done.12, f32[4,1024]{1,0:T(4,128)S(1)} %copy-done.10, f32[1024,1024,4]{1,0,2:T(8,128)S(1)} %bitcast.152, pred[1024,1024]{0,1:T(8,128)(4,1)S(1)} %iota_compare_fusion), kind=kOutput, calls=%fused_computation.72 | convolution fusion | flops 1094844416 | bytes 19169280 | tf_op jit(solution)/shard_map/kgts,tkgd->skd/dot_general | solution.py:37
  291.4 10.9 %fusion = (f32[4,1024]{1,0:T(4,128)}, f32[1024,1024,4]{1,0,2:T(8,128)}) fusion(f32[4,1024]{1,0:T(4,128)} %fusion.7, f32[4,1024]{1,0:T(4,128)} %copy-done.9, f32[1024,1024,4]{1,0,2:T(8,128)S(1)} %bitcast.152, pred[1024,1024]{0,1:T(8,128)(4,1)S(1)} %iota_compare_fusion, bf16[1024,4,128]{2,0,1:T(8,128)(2,1)} %copy-done.22, bf16[1024,1,6,128]{0,3,2,1:T(8,128)(2,1)} %bitcast.156), kind=kOutput, calls=%fused_computation.3 | convolution fusion | flops 1098903552 | bytes 35962880 | tf_op jit(solution)/shard_map/tkgd,skd->kgts/dot_general | solution.py:32
  302.3 9.2 %fusion.9 = bf16[4,1024,1024]{1,2,0:T(8,128)(2,1)S(1)} fusion(f32[1024,1024,4]{1,0,2:T(8,128)} %get-tuple-element.13, f32[4,1024]{1,0:T(4,128)} %get-tuple-element.12, f32[4,1024]{1,0:T(4,128)} %fusion.7, f32[4,1024]{1,0:T(4,128)} %copy-done.9, f32[1024,1024,4]{1,0,2:T(8,128)S(1)} %bitcast.152, pred[1024,1024]{0,1:T(8,128)(4,1)S(1)} %iota_compare_fusion), kind=kLoop, calls=%fused_computation.33 | loop fusion | flops 33554432 | bytes 43040768 | tf_op jit(solution)/shard_map/reshape.20
  316.1 9.0 %convolution_convert_fusion.3 = bf16[1024,4096]{1,0:T(8,128)(2,1)} fusion(bf16[1024,768]{0,1:T(8,128)(2,1)S(1)} %bitcast.153, bf16[4096,768]{1,0:T(8,128)(2,1)S(1)} %bitcast.161), kind=kOutput, calls=%fused_computation.42 | convolution fusion | flops 6446645248 | bytes 16252928 | tf_op jit(solution)/shard_map/tc,dc->td/dot_general | solution.py:72
  325.8 12.3 %convolution_convert_fusion.4 = bf16[4096,768]{1,0:T(8,128)(2,1)} fusion(bf16[1024,768]{0,1:T(8,128)(2,1)S(1)} %bitcast.154, bf16[1024,4096]{1,0:T(8,128)(2,1)} %param.14, f32[4096]{0:T(1024)S(1)} %copy-done.8, f32[1024]{0:T(1024)S(1)} %copy-done.17, f32[1024]{0:T(1024)S(1)} %copy-done.19), kind=kOutput, calls=%fused_computation.52 | convolution fusion | flops 6466568192 | bytes 16277504 | tf_op jit(solution)/shard_map/td,tc->dc/dot_general | solution.py:71
  338.2 19.9 %fusion.27 = bf16[4,128,4096]{2,1,0:T(8,128)(2,1)} fusion(f32[1024,4096]{1,0:T(8,128)} %multiply_add_fusion, bf16[1024,1,6,128]{0,3,2,1:T(8,128)(2,1)} %bitcast.157, f32[4,1024]{1,0:T(4,128)S(1)} %copy-done.13, f32[4,1024]{1,0:T(4,128)S(1)} %copy-done.11, f32[1024,1024,4]{1,0,2:T(8,128)} %copy-done, pred[1024,1024]{0,1:T(8,128)(4,1)S(1)} %iota_compare_fusion), kind=kOutput, calls=%fused_computation.53 | convolution fusion | flops 5396496384 | bytes 39092224 | tf_op jit(solution)/shard_map/thz,te->hze/dot_general | solution.py:69
  358.0 85.6 %all-reduce.5.cloned.1.call-done = bf16[1024,4096]{1,0:T(8,128)(2,1)} async-done(((bf16[1024,4096]{1,0:T(8,128)(2,1)}), bf16[1024,4096]{1,0:T(8,128)(2,1)}) %all-reduce.5.cloned.1.call-update) | async-done | bytes 8388624 | tf_op jit(solution)/shard_map/psum | solution.py:73
  443.6 8.9 %fusion.4 = (f32[1024]{0:T(1024)S(1)}, f32[1024]{0:T(1024)S(1)}) fusion(bf16[1024,4096]{1,0:T(8,128)(2,1)} %all-reduce.5.cloned.1.call-done, f32[4096]{0:T(1024)S(1)} %copy-done.8, f32[1024]{0:T(1024)S(1)} %copy-done.19, f32[1024]{0:T(1024)S(1)} %copy-done.17, bf16[1024,4096]{1,0:T(8,128)(2,1)} %param.14), kind=kLoop, calls=%fused_computation.10 | loop fusion | flops 33552384 | bytes 16809984 | tf_op jit(solution)/shard_map/reduce_sum | solution.py:15
  452.6 15.0 %add_convert_fusion = bf16[1024,4096]{1,0:T(8,128)(2,1)} fusion(f32[1024,4096]{1,0:T(8,128)} %multiply_add_fusion, bf16[1024,4096]{1,0:T(8,128)(2,1)S(1)} %copy-done.3, bf16[1024,4096]{1,0:T(8,128)(2,1)} %param.14, f32[1024]{0:T(1024)S(1)} %broadcast_multiply_fusion, f32[1024]{0:T(1024)S(1)} %broadcast_multiply_fusion.1, f32[4096]{0:T(1024)S(1)} %copy-done.8, ...), kind=kLoop, calls=%fused_computation.7 | loop fusion | flops 46137344 | bytes 41975808 | tf_op jit(solution)/shard_map/convert_element_type | solution.py:74
  (73 shorter events, 10.8 us)
Async XLA Ops:
  7.2 242.1 %all-reduce.3.cloned.1.call-start = ((), (), s32[]{:S(2)}) async-start(), calls=%async_computation | async-start | bytes 16777216 | tf_op jit(solution)/shard_map/psum | solution.py:61
  7.9 23.4 %copy-start.1 = (bf16[1024,4096]{1,0:T(8,128)(2,1)S(1)}, bf16[1024,4096]{1,0:T(8,128)(2,1)}, u32[]{:S(2)}) copy-start(bf16[1024,4096]{1,0:T(8,128)(2,1)} %param.15) | copy-start | bytes 25165828
  7.9 23.4 %copy-start.14 = (f32[1024]{0:T(1024)S(1)}, f32[1024]{0:T(1024)}, u32[]{:S(2)}) copy-start(f32[1024]{0:T(1024)} %param.18) | copy-start | bytes 12292
  7.9 23.4 %copy-start.15 = (f32[1024]{0:T(1024)S(1)}, f32[1024]{0:T(1024)}, u32[]{:S(2)}) copy-start(f32[1024]{0:T(1024)} %param.19) | copy-start | bytes 12292
  7.9 23.4 %copy-start.21 = (bf16[4096,1792]{1,0:T(8,128)(2,1)S(1)}, bf16[4096,1792]{1,0:T(8,128)(2,1)}, u32[]{:S(2)}) copy-start(bf16[4096,1792]{1,0:T(8,128)(2,1)} %param.24) | copy-start | bytes 44040196
  128.0 315.6 %all-reduce.5.cloned.1.call-start = ((), (), s32[]{:S(2)}) async-start(), calls=%async_computation.1 | async-start | bytes 16777216 | tf_op jit(solution)/shard_map/psum | solution.py:73
  155.6 24.0 %copy-start.20 = (bf16[4096]{0:T(1024)(128)(2,1)S(1)}, bf16[4096]{0:T(1024)(128)(2,1)}, u32[]{:S(2)}) copy-start(bf16[4096]{0:T(1024)(128)(2,1)} %param.20) | copy-start | bytes 24580
  155.6 24.0 %copy-start.16 = (f32[1024]{0:T(1024)S(1)}, f32[1024]{0:T(1024)}, u32[]{:S(2)}) copy-start(f32[1024]{0:T(1024)} %param.16) | copy-start | bytes 12292
  155.7 24.0 %copy-start.18 = (f32[1024]{0:T(1024)S(1)}, f32[1024]{0:T(1024)}, u32[]{:S(2)}) copy-start(f32[1024]{0:T(1024)} %param.17) | copy-start | bytes 12292
  179.6 12.0 %copy-start.7 = (f32[4096]{0:T(1024)}, f32[4096]{0:T(1024)S(1)}, u32[]{:S(2)}) copy-start(f32[4096]{0:T(1024)S(1)} %convert_element_type.128) | copy-start | bytes 49156
  195.1 5.7 %copy-start = (f32[1024,1024,4]{1,0,2:T(8,128)}, f32[1024,1024,4]{1,0,2:T(8,128)S(1)}, u32[]{:S(2)}) copy-start(f32[1024,1024,4]{1,0,2:T(8,128)S(1)} %get-tuple-element.11) | copy-start | bytes 50331652
  195.1 10.0 %copy-start.9 = (f32[4,1024]{1,0:T(4,128)}, f32[4,1024]{1,0:T(4,128)S(1)}, u32[]{:S(2)}) copy-start(f32[4,1024]{1,0:T(4,128)S(1)} %get-tuple-element.10) | copy-start | bytes 49156
  249.3 8.9 %copy-start.2 = (bf16[1024,4096]{1,0:T(8,128)(2,1)S(1)}, bf16[1024,4096]{1,0:T(8,128)(2,1)}, u32[]{:S(2)}) copy-start(bf16[1024,4096]{1,0:T(8,128)(2,1)} %all-reduce.3.cloned.1.call-done) | copy-start | bytes 25165828
  258.2 26.9 %slice-start = ((s8[16777216]{0:T(1024)(128)(4,1)}), s8[4194304]{0:T(1024)(128)(4,1)S(1)}, s32[]{:S(2)}) async-start(s8[16777216]{0:T(1024)(128)(4,1)} %bitcast.151), calls=%async_computation.2 | async-start | bytes 8388608
  258.2 26.9 %slice-start.1 = ((s8[16777216]{0:T(1024)(128)(4,1)}), s8[4194304]{0:T(1024)(128)(4,1)S(1)}, s32[]{:S(2)}) async-start(s8[16777216]{0:T(1024)(128)(4,1)} %bitcast.151), calls=%async_computation.3 | async-start | bytes 8388608
  274.6 10.5 %slice-start.2 = ((s8[16777216]{0:T(1024)(128)(4,1)}), s8[4194304]{0:T(1024)(128)(4,1)S(1)}, s32[]{:S(2)}) async-start(s8[16777216]{0:T(1024)(128)(4,1)} %bitcast.151), calls=%async_computation.4 | async-start | bytes 8388608
  274.6 10.5 %slice-start.3 = ((s8[16777216]{0:T(1024)(128)(4,1)}), s8[4194304]{0:T(1024)(128)(4,1)S(1)}, s32[]{:S(2)}) async-start(s8[16777216]{0:T(1024)(128)(4,1)} %bitcast.151), calls=%async_computation.5 | async-start | bytes 8388608
  274.6 10.5 %copy-start.10 = (f32[4,1024]{1,0:T(4,128)S(1)}, f32[4,1024]{1,0:T(4,128)}, u32[]{:S(2)}) copy-start(f32[4,1024]{1,0:T(4,128)} %copy-done.9) | copy-start | bytes 49156
  274.6 10.5 %copy-start.12 = (f32[4,1024]{1,0:T(4,128)S(1)}, f32[4,1024]{1,0:T(4,128)}, u32[]{:S(2)}) copy-start(f32[4,1024]{1,0:T(4,128)} %fusion.7) | copy-start | bytes 49156
  302.3 9.2 %copy-start.5 = (bf16[1024,768]{0,1:T(8,128)(2,1)S(1)}, bf16[1024,768]{0,1:T(8,128)(2,1)}, u32[]{:S(2)}) copy-start(bf16[1024,768]{0,1:T(8,128)(2,1)} %copy-done.4) | copy-start | bytes 4718596
  311.6 4.4 slice-start.4
  325.8 12.4 %copy-start.11 = (f32[4,1024]{1,0:T(4,128)S(1)}, f32[4,1024]{1,0:T(4,128)}, u32[]{:S(2)}) copy-start(f32[4,1024]{1,0:T(4,128)} %copy-done.9) | copy-start | bytes 49156
  325.8 12.4 %copy-start.13 = (f32[4,1024]{1,0:T(4,128)S(1)}, f32[4,1024]{1,0:T(4,128)}, u32[]{:S(2)}) copy-start(f32[4,1024]{1,0:T(4,128)} %fusion.7) | copy-start | bytes 49156
  443.6 8.9 %copy-start.3 = (bf16[1024,4096]{1,0:T(8,128)(2,1)S(1)}, bf16[1024,4096]{1,0:T(8,128)(2,1)}, u32[]{:S(2)}) copy-start(bf16[1024,4096]{1,0:T(8,128)(2,1)} %all-reduce.5.cloned.1.call-done) | copy-start | bytes 25165828
  (7 other events, 12.4 us)
Sparse Core Ops, SparseCore 0:
  128.1 121.0 all-reduce.2
  325.2 118.3 all-reduce.4
where the time goes:
time: 482 us; the launch traced here: 475 us
  matrix products  284 us (59%)
  waiting for transfers between devices  105 us (22%)
  other arithmetic  63.9 us (13%)
  between operations  14.8 us (3%)
  local copies, waits for them, and re-layouts  7.55 us (2%)
    psum x1, waiting for transfers between devices, device_step(): d_norm_x = lax.psum(part_x.astype(jnp.bfloat16), 'tp').astype(jnp.float32)  85.6 us
    dot_general x1, matrix products, device_step(): jnp.einsum('tf,df->td', d_gate, w_gate, preferred_element_type=jnp.float32)  29.4 us
    dot_general x1, matrix products, device_step(): jnp.einsum('td,tf->df', norm_h, d_gate, preferred_element_type=jnp.float32)  27.3 us
    dot_general x1, matrix products, device_step(): jnp.einsum('tf,df->td', d_up, w_up, preferred_element_type=jnp.float32)  27.1 us
    dot_general x1, matrix products, device_step(): jnp.einsum('td,tf->df', norm_h, d_up, preferred_element_type=jnp.float32)  24.9 us
    dot_general x1, matrix products, device_step(): jnp.einsum('tf,te->fe', hidden, d_out, preferred_element_type=jnp.float32)  24 us
    dot_general x1, matrix products, device_step(): jnp.dot(norm_h, w_up, preferred_element_type=jnp.float32)  23.4 us
    dot_general x1, matrix products, device_step(): jnp.einsum('te,fe->tf', d_out, w_down, preferred_element_type=jnp.float32)  22.9 us
  transfers between devices with their start and end apart: 2, of which 2 were waited for; matrix products, arithmetic and copies ran while one was open for 27% of the time, Pallas kernels for 0%

commit v1 on v0

v1 whole, which is shorter than its diff:
```python
import functools

import jax
import jax.numpy as jnp
from jax import lax
from jax.experimental import pallas as pl
from jax.experimental.pallas import tpu as pltpu
from jax.sharding import PartitionSpec as P

F32 = jnp.float32
BF16 = jnp.bfloat16
VMEM_LIMIT = 62 * 1024 * 1024
ANY = pl.BlockSpec(memory_space=pl.ANY)
IN_VMEM = pl.BlockSpec(memory_space=pltpu.VMEM)


def dot(lhs, rhs, lhs_dim, rhs_dim):
    return lax.dot_general(lhs, rhs, (((lhs_dim,), (rhs_dim,)), ((), ())), preferred_element_type=F32)


def resident(shape):
    return pl.BlockSpec(shape, lambda i: (0,) * len(shape), pipeline_mode=pl.Buffered(1))


def shape_of(shape, dtype=BF16):
    return jax.ShapeDtypeStruct(shape, dtype)


def params(**kw):
    return pltpu.CompilerParams(vmem_limit_bytes=VMEM_LIMIT, **kw)


def normed(src, mean, rstd, gain):
    return (((src.astype(F32) - mean) * rstd) * gain.astype(F32)).astype(BF16)


def mlp_body(h_ref, st_ref, gain_ref, do_ref, wg_ref, wu_ref, wd_ref, hid_ref, dg_ref, du_ref, n_ref):
    rows = h_ref.shape[0]

    @pl.when(pl.program_id(0) == 0)
    def _():
        @pl.loop(0, rows // 128)
        def _(i):
            r = pl.ds(pl.multiple_of(i * 128, 128), 128)
            n_ref[r, :] = normed(h_ref[r, :], st_ref[r, 0:1], st_ref[r, 1:2], gain_ref[...])

    gate = dot(n_ref[...], wg_ref[...], 1, 0).astype(BF16).astype(F32)
    up = dot(n_ref[...], wu_ref[...], 1, 0).astype(BF16).astype(F32)
    d_hid = dot(do_ref[...], wd_ref[...], 1, 1).astype(BF16).astype(F32)
    sig = jax.nn.sigmoid(gate)
    act = gate * sig
    hid_ref[...] = (act * up).astype(BF16)
    dg_ref[...] = (d_hid * up * sig * (1.0 + gate * (1.0 - sig))).astype(BF16)
    du_ref[...] = (d_hid * act).astype(BF16)


def mlp_grads(h, stats, gain, d_out, wg, wu, wd, block=256):
    t, d = h.shape
    f = wg.shape[1]
    col = lambda n: pl.BlockSpec((n, block), lambda i: (0, i))
    return pl.pallas_call(
        mlp_body,
        grid=(f // block,),
        in_specs=[resident((t, d)), resident(stats.shape), resident(gain.shape), resident((t, d)),
                  col(d), col(d), pl.BlockSpec((block, d), lambda i: (i, 0))],
        out_specs=[col(t)] * 3 + [resident((t, d))],
        out_shape=[shape_of((t, f))] * 3 + [shape_of((t, d))],
        compiler_params=params(),
        name="mlp_grads",
    )(h, stats, gain, d_out, wg, wu, wd)


def part_body(dg_ref, du_ref, wg_ref, wu_ref, out_ref):
    out_ref[...] = (dot(dg_ref[...], wg_ref[...], 1, 1) + dot(du_ref[...], wu_ref[...], 1, 1)).astype(BF16)


def mlp_part(dg, du, wg, wu, block=512):
    t, f = dg.shape
    d = wg.shape[0]
    return pl.pallas_call(
        part_body,
        grid=(d // block,),
        in_specs=[resident((t, f)), resident((t, f))] + [pl.BlockSpec((block, f), lambda i: (i, 0))] * 2,
        out_specs=pl.BlockSpec((t, block), lambda i: (0, i)),
        out_shape=shape_of((t, d)),
        compiler_params=params(),
        name="mlp_part",
    )(dg, du, wg, wu)


def attention_body(qkv_ref, do_ref, o_ref, dqkv_ref, dk_acc, dv_acc, *, group, hd, chunk):
    total = qkv_ref.shape[0]
    chunks = total // chunk
    scale = hd ** -0.5

    @pl.when(pl.program_id(0) == 0)
    def _():
        dk_acc[...] = jnp.zeros_like(dk_acc)
        dv_acc[...] = jnp.zeros_like(dv_acc)

    for c in range(chunks):
        @pl.when(pl.program_id(0) == chunks - 1 - c)
        def _():
            kv = (c + 1) * chunk
            mine = slice(c * chunk, kv)
            keys = qkv_ref[0:kv, group * hd:(group + 1) * hd]
            vals = qkv_ref[0:kv, (group + 1) * hd:(group + 2) * hd]
            q_pos = c * chunk + lax.broadcasted_iota(jnp.int32, (chunk, kv), 0)
            causal = q_pos >= lax.broadcasted_iota(jnp.int32, (chunk, kv), 1)
            for h in range(group):
                cols = slice(h * hd, (h + 1) * hd)
                q = qkv_ref[mine, cols]
                do = do_ref[:, cols]
                s = jnp.where(causal, dot(q, keys, 1, 1) * scale, -1e30)
                e = jnp.exp(s - jnp.max(s, axis=1, keepdims=True))
                p = e * (1.0 / jnp.sum(e, axis=1, keepdims=True))
                p_low = p.astype(BF16)
                o_ref[:, cols] = dot(p_low, vals, 1, 0).astype(BF16)
                dp = dot(do, vals, 1, 1)
                row_dot = jnp.sum(p * dp, axis=1, keepdims=True)
                ds = (p * (dp - row_dot) * scale).astype(BF16)
                dqkv_ref[:, cols] = dot(ds, keys, 1, 0).astype(BF16)
                dk_acc[:, 0:kv] += dot(q, ds, 0, 0)
                dv_acc[:, 0:kv] += dot(do, p_low, 0, 0)
            dqkv_ref[:, group * hd:(group + 1) * hd] = dk_acc[:, mine].T.astype(BF16)
            dqkv_ref[:, (group + 1) * hd:(group + 2) * hd] = dv_acc[:, mine].T.astype(BF16)


def attention(qkv, d_heads, hd, chunk=256):
    t, c = qkv.shape
    group = c // hd - 2
    n = t // chunk
    back = lambda w: pl.BlockSpec((chunk, w), lambda i: (n - 1 - i, 0))
    return pl.pallas_call(
        functools.partial(attention_body, group=group, hd=hd, chunk=chunk),
        grid=(n,),
        in_specs=[resident((t, c)), back(group * hd)],
        out_specs=[back(group * hd), back(c)],
        out_shape=[shape_of((t, group * hd)), shape_of((t, c))],
        scratch_shapes=[pltpu.VMEM((hd, t), F32), pltpu.VMEM((hd, t), F32)],
        compiler_params=params(),
        name="attention",
    )(qkv, d_heads)


CORE, XN, YN, DIAG = 1, 2, 4, 6
ORDER = (DIAG, XN, YN, 0)


def exchange_scratch(rows, d, base_dtype):
    half = rows // 2
    return [
        pltpu.VMEM((4, rows, d), BF16),
        pltpu.VMEM((4, rows, d), BF16),
        pltpu.VMEM((2, half, d), BF16),
        pltpu.VMEM((2, rows, d), BF16),
        pltpu.VMEM((rows, d), BF16),
        pltpu.VMEM((rows, d), BF16),
        pltpu.VMEM((rows, d), base_dtype),
        pltpu.VMEM((rows, d), F32),
        pltpu.SemaphoreType.DMA((8,)),
        pltpu.SemaphoreType.DMA((32,)),
        pltpu.SemaphoreType.DMA((32,)),
    ]


class Exchange:
    def __init__(self, rows, part, z, base, base_row, st, st_col, gain, full, own, scratch):
        self.rows, self.half = rows, rows // 2
        self.part, self.z, self.base, self.base_row = part, z, base, base_row
        self.st, self.st_col, self.gain, self.full, self.own = st, st_col, gain, full, own
        (self.from_core, self.sums, self.via, self.mine, self.res, self.zv, self.bv, self.resf,
         self.lsem, self.ssem, self.rsem) = scratch
        self.me = lax.axis_index("tp")

    def peer(self, rel):
        return lax.bitwise_xor(self.me, rel)

    def block(self, rel, lo=0, n=None):
        n = self.rows if n is None else n
        return pl.ds(pl.multiple_of(self.peer(rel) * self.rows + lo, 16), n)

    def remote(self, k, src, dst, rel):
        return pltpu.make_async_remote_copy(
            src_ref=src, dst_ref=dst, send_sem=self.ssem.at[k], recv_sem=self.rsem.at[k],
            device_id={"tp": self.peer(rel)}, device_id_type=pl.DeviceIdType.MESH)

    def core_copy(self, j):
        return self.remote(j, self.part.at[self.block(ORDER[j] ^ CORE)], self.from_core.at[j], CORE)

    def local_copy(self, j):
        return pltpu.make_async_copy(self.part.at[self.block(ORDER[j])], self.sums.at[j], self.lsem.at[j])

    def side_copies(self):
        r = self.rows
        at = self.me * r if self.base_row is None else self.base_row
        return (pltpu.make_async_copy(self.z.at[self.block(0)], self.zv, self.lsem.at[4]),
                pltpu.make_async_copy(self.base.at[pl.ds(at, r)], self.bv, self.lsem.at[5]))

    def scatter_copy(self, k):
        lo, hi = pl.ds(0, self.half), pl.ds(self.half, self.half)
        src, dst, rel = {
            4: (self.sums.at[0, lo], self.via.at[0], XN),
            5: (self.sums.at[0, hi], self.via.at[1], YN),
            6: (self.sums.at[1, lo], self.mine.at[0, lo], XN),
            7: (self.sums.at[2, hi], self.mine.at[1, hi], YN),
            8: (self.sums.at[1, hi], self.mine.at[0, hi], XN),
            9: (self.sums.at[2, lo], self.mine.at[1, lo], YN),
        }[k]
        return self.remote(k, src, dst, rel)

    def gather_copy(self, k):
        n = self.half
        src_rel, lo, cnt, to, from_res = {
            10: (0, 0, n, XN, True), 11: (0, n, n, XN, True),
            12: (0, n, n, YN, True), 13: (0, 0, n, YN, True),
            14: (0, 0, 2 * n, CORE, True),
            15: (YN, n, n, XN, False), 16: (XN, 0, n, YN, False),
            17: (XN, 0, n, CORE, False), 18: (XN, n, n, CORE, False),
            19: (YN, n, n, CORE, False), 20: (YN, 0, n, CORE, False),
            21: (DIAG, n, n, CORE, False), 22: (DIAG, 0, n, CORE, False),
        }[k]
        dst = self.full.at[self.block(src_rel, lo, cnt)]
        return self.remote(k, self.res.at[pl.ds(lo, cnt)] if from_res else dst, dst, to)

    def start(self):
        barrier = pltpu.get_barrier_semaphore()
        for rel in (CORE, XN, YN):
            pl.semaphore_signal(barrier, inc=1, device_id={"tp": self.peer(rel)}, device_id_type=pl.DeviceIdType.MESH)
        pl.semaphore_wait(barrier, 3)
        for j in range(4):
            self.core_copy(j).start()
            self.local_copy(j).start()
        for c in self.side_copies():
            c.start()

    def add(self, dst, src):
        n = dst.shape[0]

        @pl.loop(0, n // 16)
        def _(i):
            r = pl.ds(pl.multiple_of(i * 16, 16), 16)
            dst[r, :] = (dst[r, :].astype(F32) + src[r, :].astype(F32)).astype(BF16)

    def chip_sums(self):
        for j in range(4):
            self.local_copy(j).wait()
            self.core_copy(j).wait_recv()
            self.add(self.sums.at[j], self.from_core.at[j])
            for k in {0: (4, 5), 1: (6,), 2: (7,), 3: ()}[j]:
                self.scatter_copy(k).start()

    def forward_sums(self):
        lo, hi = pl.ds(0, self.half), pl.ds(self.half, self.half)
        self.scatter_copy(5).wait_recv()
        self.add(self.sums.at[1, hi], self.via.at[1])
        self.scatter_copy(8).start()
        self.scatter_copy(4).wait_recv()
        self.add(self.sums.at[2, lo], self.via.at[0])
        self.scatter_copy(9).start()

    def norm_and_send(self):
        for k in (6, 7, 8, 9):
            self.scatter_copy(k).wait_recv()
        for c in self.side_copies():
            c.wait()
        gain = self.gain[...].astype(F32)
        base = self.me * self.rows

        @pl.loop(0, self.rows // 16)
        def _(i):
            r = pl.ds(pl.multiple_of(i * 16, 16), 16)
            g = pl.ds(pl.multiple_of(base + i * 16, 16), 16)
            mean = self.st[g, self.st_col:self.st_col + 1]
            rstd = self.st[g, self.st_col + 1:self.st_col + 2]
            grad = self.sums[3, r, :].astype(F32) + self.mine[0, r, :].astype(F32) + self.mine[1, r, :].astype(F32)
            zh = (self.zv[r, :].astype(F32) - mean) * rstd
            u = grad * gain
            mean_u = jnp.mean(u, axis=1, keepdims=True)
            mean_p = jnp.mean(u * zh, axis=1, keepdims=True)
            out = self.bv[r, :].astype(F32) + rstd * (u - mean_u - zh * mean_p)
            self.resf[r, :] = out
            self.res[r, :] = out.astype(BF16)
        for k in (10, 12, 11, 13, 14):
            self.gather_copy(k).start()
        self.keep()[0].start()
        if self.own is not None:
            self.keep()[1].start()

    def keep(self):
        c = [pltpu.make_async_copy(self.res, self.full.at[self.block(0)], self.lsem.at[6])]
        if self.own is not None:
            c.append(pltpu.make_async_copy(self.resf, self.own, self.lsem.at[7]))
        return c

    def forward_first(self):
        self.gather_copy(10).wait_recv()
        self.gather_copy(16).start()
        self.gather_copy(12).wait_recv()
        self.gather_copy(15).start()
        self.gather_copy(17).start()
        self.gather_copy(19).start()

    def forward_second(self):
        self.gather_copy(11).wait_recv()
        self.gather_copy(18).start()
        self.gather_copy(13).wait_recv()
        self.gather_copy(20).start()

    def finish(self):
        self.gather_copy(15).wait_recv()
        self.gather_copy(21).start()
        self.gather_copy(16).wait_recv()
        self.gather_copy(22).start()
        for k in (14, 17, 18, 19, 20, 21, 22):
            self.gather_copy(k).wait_recv()
        for j in range(4):
            self.core_copy(j).wait_send()
        for k in range(4, 10):
            self.scatter_copy(k).wait_send()
        for k in range(10, 23):
            self.gather_copy(k).wait_send()
        for c in self.keep():
            c.wait()

    def events(self):
        return [self.chip_sums, self.forward_sums, self.norm_and_send, self.forward_first, self.forward_second,
                self.finish]


def run_phases(ex, phases, when):
    events = list(zip(when, ex.events()))
    ex.start()
    done = 0
    for body, steps, in_specs, out_specs, refs in phases:
        here = [(w - done, e) for w, e in events if done <= w < done + steps]

        def step(*tiles, body=body, here=here):
            for w, e in here:
                pl.when(pl.program_id(0) == w)(e)
            body(*tiles)

        pltpu.emit_pipeline(step, grid=(steps,), in_specs=in_specs, out_specs=out_specs)(*refs)
        done += steps
    for w, e in events:
        if w >= done:
            e()


def rows_spec(n, w):
    return pl.BlockSpec((n, w), lambda i: (i, 0))


def cols_spec(h, n):
    return pl.BlockSpec((h, n), lambda i: (0, i))


def first_body(part, z, base, st, gain_h, gain_x, n, dg, du, x, wqkv,
               full, own, dwg, dwu, nx, qkv, dgv, duv, wv, wsem, *scratch, rows, when):
    t, d = z.shape
    f = dg.shape[1]
    c = wqkv.shape[1]
    ex = Exchange(rows, part, z, base, None, st, 0, gain_h, full, own, scratch)
    loads = [pltpu.make_async_copy(s, v, wsem.at[i]) for i, (s, v) in enumerate(((dg, dgv), (du, duv), (wqkv, wv)))]
    for l in loads:
        l.start()
    for l in loads:
        l.wait()

    def weight_grads(n_t, g_t, u_t):
        g_t[...] = dot(n_t[...], dgv[...], 0, 0).astype(BF16)
        u_t[...] = dot(n_t[...], duv[...], 0, 0).astype(BF16)

    def project(x_t, s_t, n_t, q_t):
        n_t[...] = normed(x_t[...], s_t[:, 2:3], s_t[:, 3:4], gain_x[...])
        q_t[...] = dot(n_t[...], wv[...], 1, 0).astype(BF16)

    rb = 256
    phases = [
        (weight_grads, d // 256, [cols_spec(t, 256)], [rows_spec(256, f)] * 2, (n, dwg, dwu)),
        (project, t // rb, [rows_spec(rb, d), rows_spec(rb, 4)], [rows_spec(rb, d), rows_spec(rb, c)], (x, st, nx, qkv)),
    ]
    run_phases(ex, phases, when)


def first_exchange(part, h, d_out, stats, gain_h, gain_x, n, dg, du, x, wqkv, tp):
    t, d = h.shape
    f = dg.shape[1]
    c = wqkv.shape[1]
    rows = t // tp
    return pl.pallas_call(
        functools.partial(first_body, rows=rows, when=(4, 10, 19, 26, 30, 34)),
        in_specs=[ANY, ANY, ANY, IN_VMEM, IN_VMEM, IN_VMEM, ANY, ANY, ANY, ANY, ANY],
        out_specs=[ANY] * 6,
        out_shape=[shape_of((t, d)), shape_of((rows, d), F32), shape_of((d, f)), shape_of((d, f)),
                   shape_of((t, d)), shape_of((t, c))],
        scratch_shapes=[pltpu.VMEM((t, f), BF16), pltpu.VMEM((t, f), BF16), pltpu.VMEM((d, c), BF16),
                        pltpu.SemaphoreType.DMA((3,))] + exchange_scratch(rows, d, BF16),
        compiler_params=params(collective_id=1, has_side_effects=True),
        name="first_exchange",
    )(part, h, d_out, stats, gain_h, gain_x, n, dg, du, x, wqkv)


def second_body(part, z, base, st, gain_x, hid, d_out, nx, dqkv, o, dmid,
                full, dwd, dwqkv, dwo, hidv, dqv, ov, wsem, *scratch, rows, when):
    t, d = z.shape
    f = hid.shape[1]
    c = dqkv.shape[1]
    hw = o.shape[1]
    ex = Exchange(rows, part, z, base, 0, st, 2, gain_x, full, None, scratch)
    loads = [pltpu.make_async_copy(s, v, wsem.at[i]) for i, (s, v) in enumerate(((hid, hidv), (dqkv, dqv), (o, ov)))]
    for l in loads:
        l.start()
    for l in loads:
        l.wait()

    def down(do_t, out_t):
        out_t[...] = dot(hidv[...], do_t[...], 0, 0).astype(BF16)

    def qkv_grad(n_t, out_t):
        out_t[...] = dot(n_t[...], dqv[...], 0, 0).astype(BF16)

    def out_grad(dm_t, out_t):
        out_t[...] = dot(ov[...], dm_t[...], 0, 0).astype(BF16)

    phases = [
        (down, d // 512, [cols_spec(t, 512)], [cols_spec(f, 512)], (d_out, dwd)),
        (qkv_grad, d // 512, [cols_spec(t, 512)], [rows_spec(512, c)], (nx, dwqkv)),
        (out_grad, d // 512, [cols_spec(t, 512)], [cols_spec(hw, 512)], (dmid, dwo)),
    ]
    run_phases(ex, phases, when)


def second_exchange(part, x, own, stats, gain_x, hid, d_out, nx, dqkv, o, dmid, tp):
    t, d = x.shape
    f = hid.shape[1]
    c = dqkv.shape[1]
    hw = o.shape[1]
    rows = t // tp
    return pl.pallas_call(
        functools.partial(second_body, rows=rows, when=(3, 9, 24, 25, 26, 27)),
        in_specs=[ANY, ANY, ANY, IN_VMEM, IN_VMEM, ANY, ANY, ANY, ANY, ANY, ANY],
        out_specs=[ANY] * 4,
        out_shape=[shape_of((t, d)), shape_of((f, d)), shape_of((d, c)), shape_of((hw, d))],
        scratch_shapes=[pltpu.VMEM((t, f), BF16), pltpu.VMEM((t, c), BF16), pltpu.VMEM((t, hw), BF16),
                        pltpu.SemaphoreType.DMA((3,))] + exchange_scratch(rows, d, F32),
        compiler_params=params(collective_id=2, has_side_effects=True),
        name="second_exchange",
    )(part, x, own, stats, gain_x, hid, d_out, nx, dqkv, o, dmid)


def solution(mesh):
    tp = mesh.shape["tp"]

    def device_step(x_in, h_mid, mean_x, rstd_x, mean_h, rstd_h, gain_x, gain_h, w_qkv, w_out, w_gate, w_up, w_down, d_out):
        heads, hd, d = w_out.shape
        stats = jnp.stack([mean_h, rstd_h, mean_x, rstd_x], axis=1)
        gx, gh = gain_x.reshape(1, d), gain_h.reshape(1, d)
        w_o = w_out.reshape(heads * hd, d)
        hid, d_gate, d_up, norm_h = mlp_grads(h_mid, stats, gh, d_out, w_gate, w_up, w_down)
        part_h = mlp_part(d_gate, d_up, w_gate, w_up)
        d_mid_b, own, d_w_gate, d_w_up, norm_x, qkv = first_exchange(
            part_h, h_mid, d_out, stats, gh, gx, norm_h, d_gate, d_up, x_in, w_qkv, tp)
        d_heads = jnp.einsum('te,he->th', d_mid_b, w_o, preferred_element_type=F32).astype(BF16)
        o, d_qkv = attention(qkv, d_heads, hd)
        part_x = jnp.einsum('tc,dc->td', d_qkv, w_qkv, preferred_element_type=F32).astype(BF16)
        d_x, d_w_down, d_w_qkv, d_w_out = second_exchange(
            part_x, x_in, own, stats, gx, hid, d_out, norm_x, d_qkv, o, d_mid_b, tp)
        return d_x, d_w_qkv, d_w_out.reshape(w_out.shape), d_w_gate, d_w_up, d_w_down

    row_spec = P('dp', None)
    stat_spec = P('dp')
    col_spec = P(None, 'tp')
    in_specs = (row_spec, row_spec, stat_spec, stat_spec, stat_spec, stat_spec, P(None), P(None), col_spec, P('tp', None, None), col_spec, col_spec, P('tp', None), row_spec)
    out_specs = (row_spec, P('dp', 'tp'), P(('dp', 'tp'), None, None), P('dp', 'tp'), P('dp', 'tp'), P(('dp', 'tp'), None))
    return jax.shard_map(device_step, mesh=mesh, in_specs=in_specs, out_specs=out_specs, check_vma=False)
```

time: 482 us -> 376 us (0.78); the launches traced: 475 us -> 375 us
  Pallas kernels: 0 us -> 305 us
  matrix products: 284 us -> 21.4 us
  waiting for transfers between devices: 105 us -> 0 us
  other arithmetic: 63.9 us -> 0.76 us
  local copies, waits for them, and re-layouts: 7.55 us -> 47 us
  between operations: 14.8 us -> 0.7 us
    pallas_call x0 -> x5, Pallas kernels: none -> 305 us  [the longest x1 97.7 us: first_exchange(): pl.pallas_call(functools.partial(first_body, rows=rows, when=(4, 10, 19,...]
    dot_general x18 -> x2, matrix products: 284 us -> 21.4 us  [the longest x1 11.3 us: device_step(): jnp.einsum('tc,dc->td', d_qkv, w_qkv, preferred_element_type=F32)]
    psum x2 -> x0, waiting for transfers between devices: 105 us -> none  [the longest x1 85.6 us: device_step(): d_norm_x = lax.psum(part_x.astype(jnp.bfloat16), 'tp').astype(jnp.float32)]
    unnamed x58 -> x32, local copies, waits for them, and re-layouts: 7.55 us -> 43.4 us
    reduce_sum x3 -> x0, other arithmetic: 22.1 us -> none  [the longest x2 17.8 us: norm_backward(): mean_grad = jnp.mean(scaled, axis=-1, keepdims=True)]
    add x1 -> x0, other arithmetic: 16.4 us -> none  [device_step(): d_out.astype(jnp.float32)]
    convert_element_type x3 -> x0, other arithmetic: 15.7 us -> none  [the longest x1 15 us: device_step(): (d_mid + norm_backward(d_norm_x, x_in, mean_x, rstd_x, gain_x)).astype(jn...]
    another operation x1, other arithmetic: 9.21 us -> 0.76 us  [device_step(): stats = jnp.stack([mean_h, rstd_h, mean_x, rstd_x], axis=1)]
  transfers between devices with their start and end apart: 2 -> 0, of which waited for: 2 -> 0; matrix products, arithmetic and copies ran while one was open for 27% -> 0% of each run, Pallas kernels for 0% -> 0%
where the time goes in v1:
time: 376 us; the launch traced here: 375 us
  Pallas kernels  305 us (81%)
  local copies, waits for them, and re-layouts  47 us (12%)
  matrix products  21.4 us (6%)
    pallas_call x1, Pallas kernels, first_exchange(): pl.pallas_call(functools.partial(first_body, rows=rows, when=(4, 10, 19,...  97.7 us
    pallas_call x1, Pallas kernels, second_exchange(): pl.pallas_call(functools.partial(second_body, rows=rows, when=(3, 9, 24,...  91.4 us
    pallas_call x1, Pallas kernels, mlp_grads(): pl.pallas_call(mlp_body, grid=(f // block,), in_specs=[resident((t, d)),...  61 us
    unnamed x32, local copies, waits for them, and re-layouts  43.4 us
    pallas_call x1, Pallas kernels, mlp_part(): pl.pallas_call(part_body, grid=(d // block,), in_specs=[resident((t, f)),...  37.2 us
    pallas_call x1, Pallas kernels, attention(): pl.pallas_call(functools.partial(attention_body, group=group, hd=hd, chun...  17.9 us
    dot_general x1, matrix products, device_step(): jnp.einsum('tc,dc->td', d_qkv, w_qkv, preferred_element_type=F32)  11.3 us
    dot_general x1, matrix products, device_step(): jnp.einsum('te,he->th', d_mid_b, w_o, preferred_element_type=F32)  10.1 us

profile of v1, /device:TPU:0, one launch (start us, length us, event | category | flops | bytes accessed | tf_op | source)
XLA Modules:
  0.0 375.0 jit_solution(5017494438040547445)
XLA Ops:
  0.6 1.3 reshape.25.gain_x
  1.9 1.3 reshape.24.gain_ref.gain_h
  3.2 0.8 pad_maximum_fusion
  4.0 1.0 copy.24.st_ref.st
  5.0 61.0 %mlp_grads.1 = (bf16[1024,1792]{1,0:T(8,128)(2,1)}, bf16[1024,1792]{1,0:T(8,128)(2,1)}, bf16[1024,1792]{1,0:T(8,128)(2,1)}, bf16[1024,4096]{1,0:T(8,128)(2,1)}) custom-call(bf16[1024,4096]{1,0:T(8,128)(2,1)} %z.2, f32[1024,4]{1,0:T(8,128)} %copy.24.st_ref.st, bf16[1,4096]{1,0:T(2,128)(2,1)} %reshape.24.gain_ref.gain_h, bf16[1024,4096]{1,0:T(8,128)(2,1)} %d_out.1, ...), custom_call_target="tpu_custom_call" | custom-call | tf_op jit(solution)/shard_map/mlp_grads/pallas_call | solution.py:61
  66.0 37.2 %mlp_part.1.part = bf16[1024,4096]{1,0:T(8,128)(2,1)} custom-call(bf16[1024,1792]{1,0:T(8,128)(2,1)} %get-tuple-element.22.dg_ref.dg, bf16[1024,1792]{1,0:T(8,128)(2,1)} %get-tuple-element.23.du_ref.du, bf16[4096,1792]{1,0:T(8,128)(2,1)} %wg_ref.3, bf16[4096,1792]{1,0:T(8,128)(2,1)} %wu_ref.3), custom_call_target="tpu_custom_call" | custom-call | tf_op jit(solution)/shard_map/mlp_part/pallas_call | solution.py:80
  103.2 97.7 %first_exchange.1 = (bf16[1024,4096]{1,0:T(8,128)(2,1)}, f32[128,4096]{1,0:T(8,128)}, bf16[4096,1792]{1,0:T(8,128)(2,1)}, bf16[4096,1792]{1,0:T(8,128)(2,1)}, bf...) custom-call(bf16[1024,4096]{1,0:T(8,128)(2,1)} %mlp_part.1.part, bf16[1024,4096]{1,0:T(8,128)(2,1)} %z.2, ...), custom_call_target="tpu_custom_call" | custom-call | tf_op jit(solution)/shard_map/first_exchange/pallas_call | solution.py:391
  200.9 10.1 %convolution_convert_fusion.1.do_ref = bf16[1024,512]{1,0:T(8,128)(2,1)} fusion(bf16[1024,4096]{1,0:T(8,128)(2,1)} %get-tuple-element.26.dmid, bf16[512,4096]{1,0:T(8,128)(2,1)} %bitcast.21), kind=kOutput, calls=%fused_computation.1 | convolution fusion | flops 4295491584 | bytes 13631488 | tf_op jit(solution)/shard_map/te,he->th/dot_general | solution.py:464
  211.0 17.9 %attention.1 = (bf16[1024,512]{1,0:T(8,128)(2,1)}, bf16[1024,768]{1,0:T(8,128)(2,1)}) custom-call(bf16[1024,768]{1,0:T(8,128)(2,1)} %get-tuple-element.25.qkv_ref, bf16[1024,512]{1,0:T(8,128)(2,1)} %convolution_convert_fusion.1.do_ref), custom_call_target="tpu_custom_call" | custom-call | tf_op jit(solution)/shard_map/attention/pallas_call | solution.py:134
  228.9 11.3 %convolution_convert_fusion.part = bf16[1024,4096]{1,0:T(8,128)(2,1)} fusion(bf16[1024,768]{1,0:T(8,128)(2,1)} %get-tuple-element.27.dqkv, bf16[4096,768]{1,0:T(8,128)(2,1)} %wqkv.1), kind=kOutput, calls=%fused_computation | convolution fusion | flops 6446645248 | bytes 16252928 | tf_op jit(solution)/shard_map/tc,dc->td/dot_general | solution.py:466
  240.2 91.4 %second_exchange.1 = (bf16[1024,4096]{1,0:T(8,128)(2,1)}, bf16[1792,4096]{1,0:T(8,128)(2,1)}, bf16[4096,768]{1,0:T(8,128)(2,1)}, bf16[512,4096]{1,0:T(8,128)(2,1)}) custom-call(bf16[1024,4096]{1,0:T(8,128)(2,1)} %convolution_convert_fusion.part, bf16[1024,4096]{1,0:T(8,128)(2,1)} %z.3, f32[128,4096]{1,0:T(8,128)} %get-tuple-element.28.base, ...), custom_call_target="tpu_custom_call" | custom-call | tf_op jit(solution)/shard_map/second_exchange/pallas_call | solution.py:440
  331.6 0.0 slice-start.4
  331.6 0.0 slice-start.5
  331.6 8.0 %copy.33 = bf16[1024,4096]{1,0:T(8,128)(2,1)} copy(bf16[1024,4096]{1,0:T(8,128)(2,1)} %get-tuple-element.44) | data formatting | bytes 16777216
  339.7 6.5 %copy.34 = bf16[4096,768]{1,0:T(8,128)(2,1)} copy(bf16[4096,768]{1,0:T(8,128)(2,1)} %get-tuple-element.45) | data formatting | bytes 12582912
  346.2 2.1 copy.35
  348.3 1.6 slice-done.7
  350.0 7.4 %copy.36 = bf16[4096,1792]{1,0:T(8,128)(2,1)} copy(bf16[4096,1792]{1,0:T(8,128)(2,1)S(1)} %bitcast.13) | data formatting | bytes 29360128
  357.4 1.4 slice-done.2
  358.8 1.2 slice-done.3
  360.0 7.4 %copy.37 = bf16[4096,1792]{1,0:T(8,128)(2,1)} copy(bf16[4096,1792]{1,0:T(8,128)(2,1)S(1)} %bitcast.11) | data formatting | bytes 29360128
  367.4 1.5 slice-done.10
  369.0 0.6 slice-done.11
  369.6 5.5 %copy.38 = bf16[1792,4096]{1,0:T(8,128)(2,1)} copy(bf16[1792,4096]{1,0:T(8,128)(2,1)S(1)} %bitcast.15) | data formatting | bytes 29360128
  (22 shorter events, 0.0 us)
Async XLA Ops:
  331.6 16.7 %slice-start.4 = ((s8[14680064]{0:T(1024)(128)(4,1)}), s8[4194304]{0:T(1024)(128)(4,1)S(1)}, s32[]{:S(2)}) async-start(s8[14680064]{0:T(1024)(128)(4,1)} %bitcast.12), calls=%async_computation.4 | async-start | bytes 8388608
  331.6 16.7 %slice-start.5 = ((s8[14680064]{0:T(1024)(128)(4,1)}), s8[2097152]{0:T(1024)(128)(4,1)S(1)}, s32[]{:S(2)}) async-start(s8[14680064]{0:T(1024)(128)(4,1)} %bitcast.12), calls=%async_computation.5 | async-start | bytes 4194304
  339.6 6.5 %copy-start = (bf16[512,4096]{1,0:T(8,128)(2,1)S(1)}, bf16[512,4096]{1,0:T(8,128)(2,1)}, u32[]{:S(2)}) copy-start(bf16[512,4096]{1,0:T(8,128)(2,1)} %get-tuple-element.34) | copy-start | bytes 12582916
  339.7 8.7 %slice-start.6 = ((s8[14680064]{0:T(1024)(128)(4,1)}), s8[4194304]{0:T(1024)(128)(4,1)S(1)}, s32[]{:S(2)}) async-start(s8[14680064]{0:T(1024)(128)(4,1)} %bitcast.12), calls=%async_computation.6 | async-start | bytes 8388608
  339.7 10.3 %slice-start.7 = ((s8[14680064]{0:T(1024)(128)(4,1)}), s8[4194304]{0:T(1024)(128)(4,1)S(1)}, s32[]{:S(2)}) async-start(s8[14680064]{0:T(1024)(128)(4,1)} %bitcast.12), calls=%async_computation.7 | async-start | bytes 8388608
  346.2 11.2 %slice-start = ((s8[14680064]{0:T(1024)(128)(4,1)}), s8[2097152]{0:T(1024)(128)(4,1)S(1)}, s32[]{:S(2)}) async-start(s8[14680064]{0:T(1024)(128)(4,1)} %bitcast.10), calls=%async_computation | async-start | bytes 4194304
  350.0 7.5 %slice-start.1 = ((s8[14680064]{0:T(1024)(128)(4,1)}), s8[4194304]{0:T(1024)(128)(4,1)S(1)}, s32[]{:S(2)}) async-start(s8[14680064]{0:T(1024)(128)(4,1)} %bitcast.10), calls=%async_computation.1 | async-start | bytes 8388608
  350.0 8.8 %slice-start.2 = ((s8[14680064]{0:T(1024)(128)(4,1)}), s8[4194304]{0:T(1024)(128)(4,1)S(1)}, s32[]{:S(2)}) async-start(s8[14680064]{0:T(1024)(128)(4,1)} %bitcast.10), calls=%async_computation.2 | async-start | bytes 8388608
  350.0 10.0 %slice-start.3 = ((s8[14680064]{0:T(1024)(128)(4,1)}), s8[4194304]{0:T(1024)(128)(4,1)S(1)}, s32[]{:S(2)}) async-start(s8[14680064]{0:T(1024)(128)(4,1)} %bitcast.10), calls=%async_computation.3 | async-start | bytes 8388608
  350.0 17.5 %slice-start.8 = ((s8[14680064]{0:T(1024)(128)(4,1)}), s8[4194304]{0:T(1024)(128)(4,1)S(1)}, s32[]{:S(2)}) async-start(s8[14680064]{0:T(1024)(128)(4,1)} %bitcast.14), calls=%async_computation.8 | async-start | bytes 8388608
  350.0 17.5 %slice-start.9 = ((s8[14680064]{0:T(1024)(128)(4,1)}), s8[4194304]{0:T(1024)(128)(4,1)S(1)}, s32[]{:S(2)}) async-start(s8[14680064]{0:T(1024)(128)(4,1)} %bitcast.14), calls=%async_computation.9 | async-start | bytes 8388608
  360.0 9.0 %slice-start.10 = ((s8[14680064]{0:T(1024)(128)(4,1)}), s8[4194304]{0:T(1024)(128)(4,1)S(1)}, s32[]{:S(2)}) async-start(s8[14680064]{0:T(1024)(128)(4,1)} %bitcast.14), calls=%async_computation.10 | async-start | bytes 8388608
  360.0 9.6 %slice-start.11 = ((s8[14680064]{0:T(1024)(128)(4,1)}), s8[2097152]{0:T(1024)(128)(4,1)S(1)}, s32[]{:S(2)}) async-start(s8[14680064]{0:T(1024)(128)(4,1)} %bitcast.14), calls=%async_computation.11 | async-start | bytes 4194304
